TPU v7x, 32 devices: a whole 2x2x4 slice. The times are simulated.
32 devices in a mesh: dp: 8 (over y, x, core), mp: 4 (over z).
Axes of the slice: x: 2, y: 2, z: 4, core: 2. Of those that a mesh axis runs over, the one named last changes fastest.
Arguments:
- tokens: bfloat16 [8192, 2048], P('dp'), may hold values from -6 to 6
- cotangent: bfloat16 [8192, 2048], P('dp'), may hold values from -6 to 6
- counts: int32 [8], replicated, may hold values from 1 to 1024, 5120 in all
- w_qkv: bfloat16 [2048, 3, 2048], P('dp', None, 'mp'), may hold values from -0.125 to 0.125
- w_out: bfloat16 [2048, 2048], P('mp', 'dp'), may hold values from -1 to 1
- w_fc1: bfloat16 [2048, 8192], P('dp', 'mp'), may hold values from -0.125 to 0.125
- w_fc2: bfloat16 [8192, 2048], P('mp', 'dp'), may hold values from -0.0625 to 0.0625
- ln1_gain: bfloat16 [2048], P('dp'), may hold values from 0.5 to 1.5
- ln1_bias: bfloat16 [2048], P('dp'), may hold values from -1.796875 to 1.796875
- ln2_gain: bfloat16 [2048], P('dp'), may hold values from 0.5 to 1.5
- ln2_bias: bfloat16 [2048], P('dp'), may hold values from -1.796875 to 1.796875
- qv_bias: bfloat16 [2, 2048], P(None, ('mp', 'dp')), may hold values from -1.796875 to 1.796875
- out_bias: bfloat16 [2048], P('dp'), may hold values from -1.796875 to 1.796875
- fc1_bias: bfloat16 [8192], P(('mp', 'dp')), may hold values from -1.796875 to 1.796875
- fc2_bias: bfloat16 [2048], P('dp'), may hold values from -1.796875 to 1.796875
Outputs:
- out_tokens: bfloat16 [8192, 2048], P('dp')
- grad_tokens: float32 [8192, 2048], P('dp')
- grad_w_qkv: float32 [2048, 3, 2048], P('dp', None, 'mp')
- grad_w_out: float32 [2048, 2048], P('mp', 'dp')
- grad_w_fc1: float32 [2048, 8192], P('dp', 'mp')
- grad_w_fc2: float32 [8192, 2048], P('mp', 'dp')
- grad_ln1_gain: float32 [2048], P('dp')
- grad_ln1_bias: float32 [2048], P('dp')
- grad_ln2_gain: float32 [2048], P('dp')
- grad_ln2_bias: float32 [2048], P('dp')
- grad_qv_bias: float32 [2, 2048], P(None, ('mp', 'dp'))
- grad_out_bias: float32 [2048], P('dp')
- grad_fc1_bias: float32 [8192], P(('mp', 'dp'))
- grad_fc2_bias: float32 [2048], P('dp')
Inputs may be any that keep to these rules, and one draw needn't show every extreme that they name: counts[g] is the number of live tokens of group g's sequence, at the start of its 1024 slots; the largest count equals 1024.
All inputs are finite; a program needn't handle non-finite values.
Results may differ from a plain program's by a relative error of at most 0.014.
Values may be sent and summed in bfloat16 or wider, within the bound.
A program may use at most 192 MiB of HBM per device.

v0:
```python
import math
import jax
import jax.numpy as jnp
from jax import lax
from jax.sharding import PartitionSpec as P

HEAD = 128
EPS = 1e-05
NEG = -1e30


def layer_norm(values, gain_vec, shift_vec):
    center = values - jnp.mean(values, axis=-1, keepdims=True)
    spread = jnp.mean(center * center, axis=-1, keepdims=True)
    return center * lax.rsqrt(spread + EPS) * gain_vec + shift_vec


def smooth_gate(values):
    return jax.nn.gelu(values, approximate=True)


def causal_scores(queries, key_heads, inv_root):
    row_count = queries.shape[0]
    raw_scores = (
        jnp.einsum("qhd,khd->hqk", queries, key_heads, preferred_element_type=jnp.float32)
        * inv_root
    )
    future = lax.broadcasted_iota(jnp.int32, (row_count, row_count), 1) > lax.broadcasted_iota(
        jnp.int32, (row_count, row_count), 0
    )
    return jnp.where(future[None], NEG, raw_scores)


def shards(
    tokens,
    cotangent,
    counts,
    w_qkv,
    w_out,
    w_fc1,
    w_fc2,
    ln1_gain,
    ln1_bias,
    ln2_gain,
    ln2_bias,
    qv_bias,
    out_bias,
    fc1_bias,
    fc2_bias,
):
    gathered = (
        lax.all_gather(w_qkv, "dp", axis=0, tiled=True),
        lax.all_gather(w_out, "dp", axis=1, tiled=True),
        lax.all_gather(w_fc1, "dp", axis=0, tiled=True),
        lax.all_gather(w_fc2, "dp", axis=1, tiled=True),
        lax.all_gather(ln1_gain, "dp", axis=0, tiled=True),
        lax.all_gather(ln1_bias, "dp", axis=0, tiled=True),
        lax.all_gather(ln2_gain, "dp", axis=0, tiled=True),
        lax.all_gather(ln2_bias, "dp", axis=0, tiled=True),
        lax.all_gather(qv_bias, "dp", axis=1, tiled=True),
        lax.all_gather(out_bias, "dp", axis=0, tiled=True),
        lax.all_gather(fc1_bias, "dp", axis=0, tiled=True),
        lax.all_gather(fc2_bias, "dp", axis=0, tiled=True),
    )
    whole_qkv, whole_out, whole_fc1, whole_fc2 = (
        gathered[0],
        gathered[1],
        gathered[2],
        gathered[3],
    )
    gain_one = gathered[4].astype(jnp.float32)
    shift_one = gathered[5].astype(jnp.float32)
    gain_two = gathered[6].astype(jnp.float32)
    shift_two = gathered[7].astype(jnp.float32)
    bias_qv = gathered[8].astype(jnp.float32)
    bias_out = gathered[9].astype(jnp.float32)
    bias_fc1 = gathered[10].astype(jnp.float32)
    bias_fc2 = gathered[11].astype(jnp.float32)
    seq_rows = tokens.shape[0]
    local_width = whole_qkv.shape[2]
    heads_here = local_width // HEAD
    inv_root = 1.0 / math.sqrt(HEAD)
    inputs = tokens.astype(jnp.float32)
    normed_one = layer_norm(inputs, gain_one, shift_one).astype(jnp.bfloat16)
    projected = jnp.einsum("sd,dce->sce", normed_one, whole_qkv, preferred_element_type=jnp.float32)
    queries = (
        (projected[:, 0] + bias_qv[0]).astype(jnp.bfloat16).reshape(seq_rows, heads_here, HEAD)
    )
    key_heads = projected[:, 1].astype(jnp.bfloat16).reshape(seq_rows, heads_here, HEAD)
    values = (projected[:, 2] + bias_qv[1]).astype(jnp.bfloat16).reshape(seq_rows, heads_here, HEAD)
    scores = causal_scores(queries, key_heads, inv_root)
    row_peak = jnp.max(scores, axis=-1, keepdims=True)
    exp_terms = jnp.exp(scores - row_peak)
    exp_total = jnp.sum(exp_terms, axis=-1, keepdims=True)
    log_total = row_peak + jnp.log(exp_total)
    prob_low = (exp_terms / exp_total).astype(jnp.bfloat16)
    mixed_heads = (
        jnp.einsum("hqk,khd->qhd", prob_low, values, preferred_element_type=jnp.float32)
        .astype(jnp.bfloat16)
        .reshape(seq_rows, local_width)
    )
    attn_part = jnp.dot(mixed_heads, whole_out, preferred_element_type=jnp.float32)
    residual = inputs + lax.psum(attn_part, "mp") + bias_out
    normed_two = layer_norm(residual, gain_two, shift_two).astype(jnp.bfloat16)
    preact = jnp.dot(normed_two, whole_fc1, preferred_element_type=jnp.float32) + bias_fc1
    activated = smooth_gate(preact).astype(jnp.bfloat16)
    ffn_part = jnp.dot(activated, whole_fc2, preferred_element_type=jnp.float32)
    out_tokens = (
        residual + lax.psum(ffn_part.astype(jnp.bfloat16), "mp").astype(jnp.float32) + bias_fc2
    ).astype(jnp.bfloat16)
    dp_index = lax.axis_index("dp")
    slot_ids = lax.iota(jnp.int32, counts.shape[0])
    own_count = jnp.sum(jnp.where(slot_ids == dp_index, counts, 0))
    weight_share = own_count.astype(jnp.float32) / jnp.sum(counts).astype(jnp.float32)
    live_rows = lax.iota(jnp.int32, seq_rows) < own_count
    grad_out = jnp.where(live_rows[:, None], cotangent.astype(jnp.float32), 0.0)
    grad_out_low = grad_out.astype(jnp.bfloat16)
    grad_fc2 = (
        jnp.einsum("sf,sd->fd", activated, grad_out_low, preferred_element_type=jnp.float32)
        * weight_share
    )
    grad_fc2_bias = jnp.sum(grad_out, axis=0) * weight_share
    delta_act = jnp.einsum("sd,fd->sf", grad_out_low, whole_fc2, preferred_element_type=jnp.float32)
    unused_gate, gate_back = jax.vjp(smooth_gate, preact)
    delta_pre = gate_back(delta_act)[0]
    grad_fc1_bias = jnp.sum(delta_pre, axis=0) * weight_share
    delta_pre_low = delta_pre.astype(jnp.bfloat16)
    grad_fc1 = (
        jnp.einsum("sd,sf->df", normed_two, delta_pre_low, preferred_element_type=jnp.float32)
        * weight_share
    )
    two_part = jnp.einsum("sf,df->sd", delta_pre_low, whole_fc1, preferred_element_type=jnp.float32)
    delta_two = lax.psum(two_part, "mp")
    unused_two, second_back = jax.vjp(layer_norm, residual, gain_two, shift_two)
    resid_part, gain_two_part, shift_two_part = second_back(delta_two)
    delta_resid = resid_part + grad_out
    delta_resid_low = delta_resid.astype(jnp.bfloat16)
    out_bias_part = jnp.sum(delta_resid, axis=0)
    grad_out_proj = (
        jnp.einsum("sc,sd->cd", mixed_heads, delta_resid_low, preferred_element_type=jnp.float32)
        * weight_share
    )
    delta_mixed = jnp.einsum(
        "sd,cd->sc", delta_resid_low, whole_out, preferred_element_type=jnp.float32
    )
    delta_mixed_low = delta_mixed.astype(jnp.bfloat16).reshape(seq_rows, heads_here, HEAD)
    scores_again = causal_scores(queries, key_heads, inv_root)
    prob_full = jnp.exp(scores_again - log_total)
    delta_prob = jnp.einsum(
        "qhd,khd->hqk", delta_mixed_low, values, preferred_element_type=jnp.float32
    )
    delta_scores = prob_full * (
        delta_prob - jnp.sum(prob_full * delta_prob, axis=-1, keepdims=True)
    )
    delta_scores_low = delta_scores.astype(jnp.bfloat16)
    delta_q = (
        jnp.einsum("hqk,khd->qhd", delta_scores_low, key_heads, preferred_element_type=jnp.float32)
        * inv_root
    ).reshape(seq_rows, local_width)
    delta_k = (
        jnp.einsum("hqk,qhd->khd", delta_scores_low, queries, preferred_element_type=jnp.float32)
        * inv_root
    ).reshape(seq_rows, local_width)
    delta_v = jnp.einsum(
        "hqk,qhd->khd", prob_low, delta_mixed_low, preferred_element_type=jnp.float32
    ).reshape(seq_rows, local_width)
    grad_qv = jnp.stack([jnp.sum(delta_q, axis=0), jnp.sum(delta_v, axis=0)]) * weight_share
    delta_proj = jnp.stack([delta_q, delta_k, delta_v], axis=1).astype(jnp.bfloat16)
    grad_qkv = (
        jnp.einsum("sd,sce->dce", normed_one, delta_proj, preferred_element_type=jnp.float32)
        * weight_share
    )
    one_part = jnp.einsum("sce,dce->sd", delta_proj, whole_qkv, preferred_element_type=jnp.float32)
    delta_one = lax.psum(one_part.astype(jnp.bfloat16), "mp").astype(jnp.float32)
    unused_one, first_back = jax.vjp(layer_norm, inputs, gain_one, shift_one)
    input_part, gain_one_part, shift_one_part = first_back(delta_one)
    grad_tokens = input_part + delta_resid
    stat_sums = jnp.stack(
        [gain_two_part, shift_two_part, out_bias_part, gain_one_part, shift_one_part]
    )
    stat_weighted = stat_sums * weight_share
    summed_all = (
        lax.psum_scatter(grad_qkv, "dp", scatter_dimension=0, tiled=True),
        lax.psum_scatter(grad_out_proj, "dp", scatter_dimension=1, tiled=True),
        lax.psum_scatter(grad_qv, "dp", scatter_dimension=1, tiled=True),
        lax.psum_scatter(stat_weighted[2], "dp", scatter_dimension=0, tiled=True),
        lax.psum_scatter(stat_weighted[3], "dp", scatter_dimension=0, tiled=True),
        lax.psum_scatter(stat_weighted[4], "dp", scatter_dimension=0, tiled=True),
        lax.psum_scatter(grad_fc1, "dp", scatter_dimension=0, tiled=True),
        lax.psum_scatter(grad_fc2, "dp", scatter_dimension=1, tiled=True),
        lax.psum_scatter(grad_fc1_bias, "dp", scatter_dimension=0, tiled=True),
        lax.psum_scatter(grad_fc2_bias, "dp", scatter_dimension=0, tiled=True),
        lax.psum_scatter(stat_weighted[0], "dp", scatter_dimension=0, tiled=True),
        lax.psum_scatter(stat_weighted[1], "dp", scatter_dimension=0, tiled=True),
    )
    return (
        out_tokens,
        grad_tokens,
        summed_all[0],
        summed_all[1],
        summed_all[6],
        summed_all[7],
        summed_all[4],
        summed_all[5],
        summed_all[10],
        summed_all[11],
        summed_all[2],
        summed_all[3],
        summed_all[8],
        summed_all[9],
    )


def solution(mesh):
    placed = (
        P("dp", None),
        P("dp", None),
        P(),
        P("dp", None, "mp"),
        P("mp", "dp"),
        P("dp", "mp"),
        P("mp", "dp"),
        P("dp"),
        P("dp"),
        P("dp"),
        P("dp"),
        P(None, ("mp", "dp")),
        P("dp"),
        P(("mp", "dp")),
        P("dp"),
    )
    return jax.shard_map(
        shards,
        mesh=mesh,
        in_specs=placed,
        out_specs=(
            P("dp", None),
            P("dp", None),
            P("dp", None, "mp"),
            P("mp", "dp"),
            P("dp", "mp"),
            P("mp", "dp"),
            P("dp"),
            P("dp"),
            P("dp"),
            P("dp"),
            P(None, ("mp", "dp")),
            P("dp"),
            P(("mp", "dp")),
            P("dp"),
        ),
        check_vma=False,
    )
```

profile of v0, /device:TPU:0, one launch (start us, length us, event | category | flops | bytes accessed | tf_op | source)
XLA Modules:
  0.0 1627.1 jit_solution(16595095688366546610)
XLA Ops:
  12.0 10.4 all-gather.2
  28.8 8.9 all-gather.1
  37.7 8.6 all-gather
  46.3 13.5 all-gather.13.cloned.1.call-done
  59.8 10.4 fusion.38
  79.8 8.1 fusion
  89.9 8.5 divide_convert_fusion
  112.2 9.1 all-gather.6
  129.3 8.9 all-gather.5
  147.5 254.6 %all-reduce.13.cloned.1.call-done = f32[1024,2048]{1,0:T(8,128)} async-done(((f32[1024,2048]{1,0:T(8,128)}), f32[1024,2048]{1,0:T(8,128)}) %all-reduce.13.cloned.1.call-update) | async-done | bytes 8388624 | tf_op jit(solution)/shard_map/psum | solution.py:103
  412.4 44.7 %all-gather.17.cloned.1.call-done = bf16[2048,2048]{1,0:T(8,128)(2,1)} async-done(((bf16[256,2048]{1,0:T(8,128)(2,1)}), bf16[2048,2048]{1,0:T(8,128)(2,1)}) %all-gather.17.cloned.1.call-update) | async-done | bytes 8388624 | tf_op jit(solution)/shard_map/all_gather | solution.py:54
  457.1 16.0 fusion.48
  473.1 41.7 %all-gather.19.cloned.1.call-done = bf16[2048,2048]{1,0:T(8,128)(2,1)} async-done(((bf16[2048,256]{1,0:T(8,128)(2,1)}), bf16[2048,2048]{1,0:T(8,128)(2,1)}) %all-gather.19.cloned.1.call-update) | async-done | bytes 8388624 | tf_op jit(solution)/shard_map/all_gather | solution.py:55
  514.7 20.5 %fusion.58 = (f32[2048]{0:T(1024)}, bf16[1024,2048]{1,0:T(8,128)(2,1)S(1)}) fusion(f32[1024,2048]{1,0:T(8,128)} %fusion.48, f32[2048]{0:T(1024)S(1)} %bitcast.123, bf16[2048,2048]{1,0:T(8,128)(2,1)} %all-gather.19.cloned.1.call-done, bf16[1024,2048]{1,0:T(8,128)(2,1)} %param.16, pred[1024]{0:T(1024)(128)(4,1)S(1)} %iota_compare_fusion.1), kind=kOutput, calls=%fused_computation.107 | convolution fusion | flops 8642361344 | bytes 25183232 | tf_op jit(solution)/shard_map/sd,fd->sf/dot_general | solution.py:123
  537.2 13.2 fusion.27
  551.9 16.9 %convolution_convert_fusion = bf16[1024,2048]{1,0:T(8,128)(2,1)} fusion(bf16[2048,2048]{1,0:T(8,128)(2,1)} %all-gather.19.cloned.1.call-done, f32[1024,2048]{1,0:T(8,128)} %fusion.48, f32[2048]{0:T(1024)S(1)} %bitcast.124), kind=kOutput, calls=%fused_computation.53 | convolution fusion | flops 8613003264 | bytes 20979712 | tf_op jit(solution)/shard_map/dot_general | solution.py:107
  568.8 272.7 %all-reduce.15.cloned.1.call-done = f32[1024,2048]{1,0:T(8,128)} async-done(((f32[1024,2048]{1,0:T(8,128)}), f32[1024,2048]{1,0:T(8,128)}) %all-reduce.15.cloned.1.call-update) | async-done | bytes 8388624 | tf_op jit(solution)/shard_map/psum | solution.py:133
  864.3 10.6 multiply_reduce_fusion
  874.9 12.4 multiply_convert_fusion
  902.1 11.0 bitcast_convert_fusion
  914.3 9.2 convolution_multiply_fusion.2
  923.6 17.6 %convolution_multiply_fusion = f32[2048,2048]{1,0:T(8,128)} fusion(f32[]{:T(128)S(6)} %div.63, bf16[1024,2048]{1,0:T(8,128)(2,1)} %param.16, pred[1024]{0:T(1024)(128)(4,1)S(1)} %iota_compare_fusion.1, f32[1024,2048]{1,0:T(8,128)} %fusion.48, f32[2048]{0:T(1024)S(1)} %bitcast.125), kind=kOutput, calls=%fused_computation.23 | convolution fusion | flops 8621391872 | bytes 29369348 | tf_op jit(solution)/shard_map/sf,sd->fd/dot_general | solution.py:119
  941.9 17.1 %convolution_multiply_fusion.1 = f32[2048,2048]{1,0:T(8,128)} fusion(f32[]{:T(128)S(6)} %div.63, bf16[1024,2048]{1,0:T(8,128)(2,1)} %copy-done.43, f32[1024,2048]{1,0:T(8,128)} %copy-done, f32[2048]{0:T(1024)S(1)} %bitcast.122, f32[2048]{0:T(1024)S(1)} %bitcast.98, f32[1024]{0:T(1024)S(1)} %fusion.42, f32[1024]{0:T(1024)S(1)} %broadcast_multiply_fusion.4), kind=kOutput, calls=%fused_computation.24 | convolution fusion | flops 8604614656 | bytes 29384708 | tf_op jit(solution)/shard_map/sd,sf->df/dot_general | solution.py:129
  960.3 13.7 broadcast_multiply_fusion
  974.6 8.9 all-gather.7
  986.2 242.6 %all-reduce.17.cloned.1.call-done = (bf16[1024,2048]{1,0:T(8,128)(2,1)}, bf16[1024,2048]{1,0:T(8,128)(2,1)}) async-done(((bf16[1024,2048]{1,0:T(8,128)(2,1)}, bf16[1024,2048]{1,0:T(8,128)(2,1)}), (bf16[1024,2048]{1,0:T(8,128)(2,1)}, bf16[1024,2048]{1,0:T(8,128)(2,1)})) %all-reduce.17.cloned.1.call-update) | async-done | bytes 8388624 | tf_op jit(solution)/shard_map/psum | solution.py:109
  1239.3 10.4 fusion.19
  1249.8 25.4 %all-reduce.7 = (f32[2048]{0:T(1024)S(1)}, f32[2048]{0:T(1024)S(1)}, f32[2048]{0:T(1024)S(1)}, f32[2048]{0:T(1024)S(1)}, f32[2048]{0:T(1024)S(1)}, /*index=5*/f32[2048]{0:T(1024)S(1)}, f32[2048]{0:T(1024)S(1)}) all-reduce(f32[2048]{0:T(1024)S(1)} %bitcast.111, f32[2048]{0:T(1024)S(1)} %bitcast.110, ...), channel_id=6, replica_groups=mesh['dp'=8,'mp'=4] {'dp'}, use_global_device_ids=true, to_apply=%region_26.27.clone | all-reduce | flops 14336 | bytes 114688
  1279.7 8.5 add_convert_fusion
  1288.2 115.5 %reduce-scatter.14.cloned.1.call-done = f32[2048,256]{1,0:T(8,128)} async-done(((f32[2048,2048]{1,0:T(8,128)}), f32[2048,256]{1,0:T(8,128)}) %reduce-scatter.14.cloned.1.call-update) | async-done | bytes 2097168 | tf_op jit(solution)/shard_map/reduce_scatter | solution.py:190
  1403.7 120.4 %reduce-scatter.12.cloned.1.call-done = f32[256,2048]{1,0:T(8,128)} async-done(((f32[2048,2048]{1,0:T(8,128)}), f32[256,2048]{1,0:T(8,128)}) %reduce-scatter.12.cloned.1.call-update) | async-done | bytes 2097168 | tf_op jit(solution)/shard_map/reduce_scatter | solution.py:189
  1524.0 96.0 %reduce-scatter.8.cloned.1.call-done = f32[256,3,512]{2,0,1:T(8,128)} async-done(((f32[2048,3,512]{2,0,1:T(8,128)}), f32[256,3,512]{2,0,1:T(8,128)}) %reduce-scatter.8.cloned.1.call-update) | async-done | bytes 1572880 | tf_op jit(solution)/shard_map/reduce_scatter | solution.py:183
  (191 shorter events, 124.1 us)
Async XLA Ops:
  7.2 52.6 %all-gather.13.cloned.1.call-start = ((), (), s32[]{:S(2)}) async-start(), calls=%async_computation.5 | async-start | bytes 7077888 | tf_op jit(solution)/shard_map/all_gather | solution.py:52
  9.5 93.5 %all-gather.15.cloned.1.call-start = ((), (), s32[]{:S(2)}) async-start(), calls=%async_computation.6 | async-start | bytes 2359296 | tf_op jit(solution)/shard_map/all_gather | solution.py:53
  10.3 391.8 %all-reduce.13.cloned.1.call-start = ((), (), s32[]{:S(2)}) async-start(), calls=%async_computation.7 | async-start | bytes 16777216 | tf_op jit(solution)/shard_map/psum | solution.py:103
  22.4 49.7 %copy-start.29 = (f32[1,512]{1,0:T(1,128)}, f32[1,512]{1,0:T(1,128)S(1)}, u32[]{:S(2)}) copy-start(f32[1,512]{1,0:T(1,128)S(1)} %get-tuple-element.47) | copy-start | bytes 6148
  25.3 44.9 %copy-start.21 = (f32[1024]{0:T(1024)}, f32[1024]{0:T(1024)S(1)}, u32[]{:S(2)}) copy-start(f32[1024]{0:T(1024)S(1)} %broadcast_multiply_fusion.5) | copy-start | bytes 12292
  28.8 8.9 copy-start.25
  28.8 41.5 %copy-start.23 = (f32[1024]{0:T(1024)}, f32[1024]{0:T(1024)S(1)}, u32[]{:S(2)}) copy-start(f32[1024]{0:T(1024)S(1)} %fusion.41) | copy-start | bytes 12292
  37.7 32.6 %copy-start.31 = (f32[8,1,256]{2,1,0:T(1,128)}, f32[8,1,256]{2,1,0:T(1,128)S(1)}, u32[]{:S(2)}) copy-start(f32[8,1,256]{2,1,0:T(1,128)S(1)} %convert_element_type.130) | copy-start | bytes 24580
  46.3 23.9 %copy-start.19 = (f32[8,1,256]{2,1,0:T(1,128)}, f32[8,1,256]{2,1,0:T(1,128)S(1)}, u32[]{:S(2)}) copy-start(f32[8,1,256]{2,1,0:T(1,128)S(1)} %convert_element_type.129) | copy-start | bytes 24580
  70.4 9.3 copy-start.10
  89.9 8.5 copy-start.8
  110.8 35.4 %copy-start.36 = (s32[8]{0:T(128)S(1)}, s32[8]{0:T(128)}, u32[]{:S(2)}) copy-start(s32[8]{0:T(128)} %param.17) | copy-start | bytes 100
  110.9 346.2 %all-gather.17.cloned.1.call-start = ((), (), s32[]{:S(2)}) async-start(), calls=%async_computation.8 | async-start | bytes 9437184 | tf_op jit(solution)/shard_map/all_gather | solution.py:54
  111.5 403.3 %all-gather.19.cloned.1.call-start = ((), (), s32[]{:S(2)}) async-start(), calls=%async_computation.9 | async-start | bytes 9437184 | tf_op jit(solution)/shard_map/all_gather | solution.py:55
  112.0 729.4 %all-reduce.15.cloned.1.call-start = ((), (), s32[]{:S(2)}) async-start(), calls=%async_computation.10 | async-start | bytes 16777216 | tf_op jit(solution)/shard_map/psum | solution.py:133
  138.2 318.9 %copy-start.34 = (f32[8,1,256]{2,1,0:T(1,128)}, f32[8,1,256]{2,1,0:T(1,128)S(1)}, u32[]{:S(2)}) copy-start(f32[8,1,256]{2,1,0:T(1,128)S(1)} %convert_element_type.134) | copy-start | bytes 24580
  550.5 434.4 %reduce-scatter.16.cloned.1.call-start = ((), (), s32[]{:S(2)}) async-start(), calls=%async_computation.15 | async-start | bytes 294912
  841.4 8.2 copy-start.5
  849.7 11.7 slice-start
  874.9 12.4 copy-start.7
  874.9 12.4 copy-start.30
  902.0 326.9 %all-reduce.17.cloned.1.call-start = ((), (), s32[]{:S(2)}) async-start(), calls=%async_computation.16 | async-start | bytes 16777216 | tf_op jit(solution)/shard_map/psum | solution.py:109
  913.1 375.1 %reduce-scatter.10.cloned.1.call-start = ((), (), s32[]{:S(2)}) async-start(), calls=%async_computation.12 | async-start | bytes 4718592 | tf_op jit(solution)/shard_map/reduce_scatter | solution.py:184
  923.5 480.1 %reduce-scatter.14.cloned.1.call-start = ((), (), s32[]{:S(2)}) async-start(), calls=%async_computation.14 | async-start | bytes 18874368 | tf_op jit(solution)/shard_map/reduce_scatter | solution.py:190
  941.2 582.8 %reduce-scatter.12.cloned.1.call-start = ((), (), s32[]{:S(2)}) async-start(), calls=%async_computation.13 | async-start | bytes 18874368 | tf_op jit(solution)/shard_map/reduce_scatter | solution.py:189
  959.0 661.0 %reduce-scatter.8.cloned.1.call-start = ((), (), s32[]{:S(2)}) async-start(), calls=%async_computation.11 | async-start | bytes 14155776 | tf_op jit(solution)/shard_map/reduce_scatter | solution.py:183
  974.0 9.6 copy-start.42
  974.0 10.8 copy-start.33
  974.0 260.5 %copy-start.26 = (f32[1024]{0:T(1024)S(1)}, f32[1024]{0:T(1024)}, u32[]{:S(2)}) copy-start(f32[1024]{0:T(1024)} %copy-done.25) | copy-start | bytes 12292
  1228.9 10.4 copy-start.13
  1239.2 10.4 copy-start.27
  1239.2 10.4 copy-start.28
  (26 other events, 84.7 us)
Sparse Core Ops, SparseCore 0:
  10.4 49.3 all-gather.12
  61.7 28.0 all-gather.14
  111.0 291.0 all-reduce.12
  403.8 53.2 all-gather.16
  458.8 55.8 all-gather.18
  550.6 290.8 all-reduce.14
  902.1 32.6 reduce-scatter.15
  938.0 290.8 all-reduce.16
  1232.8 50.8 reduce-scatter.9
  1287.7 115.9 reduce-scatter.13
  1407.8 116.1 reduce-scatter.11
  1527.9 92.0 reduce-scatter.7
where the time goes:
time: 1630 us
  waiting for transfers between devices  1200 us (74%)
  matrix products  190 us (12%)
  blocking collectives  96.2 us (6%)
  other arithmetic  87.9 us (5%)
  local copies, waits for them, and re-layouts  32.2 us (2%)
  between operations  17.2 us (1%)
    psum x1, waiting for transfers between devices, shards(): delta_two = lax.psum(two_part, 'mp')  273 us
    psum x1, waiting for transfers between devices, shards(): residual = inputs + lax.psum(attn_part, 'mp') + bias_out  255 us
    psum x1, waiting for transfers between devices, shards(): lax.psum(ffn_part.astype(jnp.bfloat16), 'mp').astype(jnp.float32)  243 us
    reduce_scatter x1, waiting for transfers between devices, shards(): lax.psum_scatter(grad_fc1, 'dp', scatter_dimension=0, tiled=True)  120 us
    reduce_scatter x1, waiting for transfers between devices, shards(): lax.psum_scatter(grad_fc2, 'dp', scatter_dimension=1, tiled=True)  115 us
    reduce_scatter x1, waiting for transfers between devices, shards(): lax.psum_scatter(grad_qkv, 'dp', scatter_dimension=0, tiled=True)  96 us
    all_gather x1, waiting for transfers between devices, shards(): lax.all_gather(w_fc1, 'dp', axis=0, tiled=True)  44.7 us
    all_gather x1, waiting for transfers between devices, shards(): lax.all_gather(w_fc2, 'dp', axis=1, tiled=True)  41.7 us
  transfers between devices with their start and end apart: 12, of which 9 were waited for; matrix products, arithmetic and copies ran while one was open for 12% of the time, Pallas kernels for 0%

commit v1 on v0

--- a/solution.py
+++ b/solution.py
@@ -7,6 +7,27 @@
 HEAD = 128
 EPS = 1e-05
 NEG = -1e30
+
+
+def gather_around(x, axis, dim):
+    count, index, rows = (lax.axis_size(axis), lax.axis_index(axis), x.shape[dim])
+    right = [(i, (i + 1) % count) for i in range(count)]
+    left = [(i, (i - 1) % count) for i in range(count)]
+    result = jnp.zeros((*x.shape[:dim], count * rows, *x.shape[dim + 1 :]), x.dtype)
+    result = lax.dynamic_update_slice_in_dim(result, x, index * rows, axis=dim)
+    from_left = from_right = x
+    half = count // 2
+    for turn in range(1, half + 1):
+        from_left = lax.ppermute(from_left, axis, right)
+        result = lax.dynamic_update_slice_in_dim(
+            result, from_left, (index - turn) % count * rows, axis=dim
+        )
+        if turn < count - half:
+            from_right = lax.ppermute(from_right, axis, left)
+            result = lax.dynamic_update_slice_in_dim(
+                result, from_right, (index + turn) % count * rows, axis=dim
+            )
+    return result
 
 
 def layer_norm(values, gain_vec, shift_vec):
@@ -51,7 +72,7 @@
     gathered = (
         lax.all_gather(w_qkv, "dp", axis=0, tiled=True),
         lax.all_gather(w_out, "dp", axis=1, tiled=True),
-        lax.all_gather(w_fc1, "dp", axis=0, tiled=True),
+        gather_around(w_fc1, "dp", 0),
         lax.all_gather(w_fc2, "dp", axis=1, tiled=True),
         lax.all_gather(ln1_gain, "dp", axis=0, tiled=True),
         lax.all_gather(ln1_bias, "dp", axis=0, tiled=True),

time: 1630 us -> 1580 us (0.969)
  waiting for transfers between devices: 1200 us -> 1120 us
    psum x1, waiting for transfers between devices: 255 us -> 163 us  [shards(): residual = inputs + lax.psum(attn_part, 'mp') + bias_out]
    ppermute x0 -> x7, waiting for transfers between devices: none -> 62.8 us  [the longest x4 47.7 us: gather_around(): from_left = lax.ppermute(from_left, axis, right)]
    all_gather x1 -> x0, waiting for transfers between devices: 44.7 us -> none  [shards(): lax.all_gather(w_fc1, 'dp', axis=0, tiled=True)]
  transfers between devices with their start and end apart: 12 -> 18, of which waited for: 9 -> 12; matrix products, arithmetic and copies ran while one was open for 12% -> 13% of each run, Pallas kernels for 0% -> 0%
where the time goes in v1:
time: 1580 us; the launch traced here: 1570 us
  waiting for transfers between devices  1120 us (71%)
  matrix products  187 us (12%)
  blocking collectives  104 us (7%)
  other arithmetic  87.7 us (6%)
  local copies, waits for them, and re-layouts  46.8 us (3%)
  between operations  16.9 us (1%)
    psum x1, waiting for transfers between devices, shards(): delta_two = lax.psum(two_part, 'mp')  273 us
    psum x1, waiting for transfers between devices, shards(): lax.psum(ffn_part.astype(jnp.bfloat16), 'mp').astype(jnp.float32)  243 us
    psum x1, waiting for transfers between devices, shards(): residual = inputs + lax.psum(attn_part, 'mp') + bias_out  163 us
    reduce_scatter x1, waiting for transfers between devices, shards(): lax.psum_scatter(grad_fc1, 'dp', scatter_dimension=0, tiled=True)  120 us
    reduce_scatter x1, waiting for transfers between devices, shards(): lax.psum_scatter(grad_fc2, 'dp', scatter_dimension=1, tiled=True)  116 us
    reduce_scatter x1, waiting for transfers between devices, shards(): lax.psum_scatter(grad_qkv, 'dp', scatter_dimension=0, tiled=True)  96.2 us
    ppermute x4, waiting for transfers between devices, gather_around(): from_left = lax.ppermute(from_left, axis, right)  47.7 us
    all_gather x1, waiting for transfers between devices, shards(): lax.all_gather(w_fc2, 'dp', axis=1, tiled=True)  33.6 us
  transfers between devices with their start and end apart: 18, of which 12 were waited for; matrix products, arithmetic and copies ran while one was open for 13% of the time, Pallas kernels for 0%

profile of v1, /device:TPU:0, one launch (start us, length us, event | category | flops | bytes accessed | tf_op | source)
XLA Modules:
  0.0 1571.2 jit_solution(14756623118205757407)
XLA Ops:
  12.0 10.4 all-gather.2
  28.8 8.9 all-gather.1
  37.7 8.6 all-gather
  46.3 13.5 all-gather.12.cloned.1.call-done
  59.8 10.4 fusion.38
  114.3 22.6 %collective-permute-done = bf16[256,2048]{1,0:T(8,128)(2,1)S(1)} collective-permute-done((bf16[256,2048]{1,0:T(8,128)(2,1)S(1)}, bf16[256,2048]{1,0:T(8,128)(2,1)S(1)}, u32[]{:S(2)}, u32[]{:S(2)}) %collective-permute-start) | collective-permute-done | bytes 1048608 | tf_op jit(solution)/shard_map/ppermute | solution.py:21
  139.6 23.2 %collective-permute-done.2 = bf16[256,2048]{1,0:T(8,128)(2,1)} collective-permute-done((bf16[256,2048]{1,0:T(8,128)(2,1)S(1)}, bf16[256,2048]{1,0:T(8,128)(2,1)}, u32[]{:S(2)}, u32[]{:S(2)}) %collective-permute-start.2) | collective-permute-done | bytes 1048608 | tf_op jit(solution)/shard_map/ppermute | solution.py:21
  162.8 16.0 %all-gather.6 = bf16[8,1,256]{2,1,0:T(2,128)(2,1)S(1)} all-gather(bf16[1,1,256]{2,1,0:T(2,128)(2,1)S(1)} %reshape.172), channel_id=1, replica_groups=mesh['dp'=8,'mp'=4] {'dp'}, dimensions={0}, use_global_device_ids=true | all-gather | bytes 4608 | tf_op jit(solution)/shard_map/all_gather | solution.py:83
  178.9 8.5 all-gather.3
  187.4 9.3 all-gather.5
  220.5 15.1 collective-permute-done.5
  239.6 162.6 %all-reduce.13.cloned.1.call-done = f32[1024,2048]{1,0:T(8,128)} async-done(((f32[1024,2048]{1,0:T(8,128)}), f32[1024,2048]{1,0:T(8,128)}) %all-reduce.13.cloned.1.call-update) | async-done | bytes 8388624 | tf_op jit(solution)/shard_map/psum | solution.py:124
  411.5 13.7 fusion.48
  425.1 33.6 %all-gather.16.cloned.1.call-done = bf16[2048,2048]{1,0:T(8,128)(2,1)} async-done(((bf16[2048,256]{1,0:T(8,128)(2,1)}), bf16[2048,2048]{1,0:T(8,128)(2,1)}) %all-gather.16.cloned.1.call-update) | async-done | bytes 8388624 | tf_op jit(solution)/shard_map/all_gather | solution.py:76
  458.8 20.5 %fusion.58 = (f32[2048]{0:T(1024)}, bf16[1024,2048]{1,0:T(8,128)(2,1)S(1)}) fusion(f32[1024,2048]{1,0:T(8,128)} %fusion.48, f32[2048]{0:T(1024)S(1)} %bitcast.123, bf16[2048,2048]{1,0:T(8,128)(2,1)} %all-gather.16.cloned.1.call-done, bf16[1024,2048]{1,0:T(8,128)(2,1)} %param.16, pred[1024]{0:T(1024)(128)(4,1)S(1)} %iota_compare_fusion.1), kind=kOutput, calls=%fused_computation.115 | convolution fusion | flops 8642361344 | bytes 25183232 | tf_op jit(solution)/shard_map/sd,fd->sf/dot_general | solution.py:144
  481.3 13.3 fusion.27
  496.0 16.9 %convolution_convert_fusion = bf16[1024,2048]{1,0:T(8,128)(2,1)} fusion(bf16[2048,2048]{1,0:T(8,128)(2,1)} %all-gather.16.cloned.1.call-done, f32[1024,2048]{1,0:T(8,128)} %fusion.48, f32[2048]{0:T(1024)S(1)} %bitcast.124), kind=kOutput, calls=%fused_computation.53 | convolution fusion | flops 8613003264 | bytes 20979712 | tf_op jit(solution)/shard_map/dot_general | solution.py:128
  512.9 272.7 %all-reduce.15.cloned.1.call-done = f32[1024,2048]{1,0:T(8,128)} async-done(((f32[1024,2048]{1,0:T(8,128)}), f32[1024,2048]{1,0:T(8,128)}) %all-reduce.15.cloned.1.call-update) | async-done | bytes 8388624 | tf_op jit(solution)/shard_map/psum | solution.py:154
  808.5 10.6 multiply_reduce_fusion
  819.1 12.4 multiply_convert_fusion
  846.2 11.0 bitcast_convert_fusion
  858.5 9.2 convolution_multiply_fusion.2
  867.7 17.6 %convolution_multiply_fusion = f32[2048,2048]{1,0:T(8,128)} fusion(f32[]{:T(128)S(6)} %div.63, bf16[1024,2048]{1,0:T(8,128)(2,1)} %param.16, pred[1024]{0:T(1024)(128)(4,1)S(1)} %iota_compare_fusion.1, f32[1024,2048]{1,0:T(8,128)} %fusion.48, f32[2048]{0:T(1024)S(1)} %bitcast.125), kind=kOutput, calls=%fused_computation.23 | convolution fusion | flops 8621391872 | bytes 29369348 | tf_op jit(solution)/shard_map/sf,sd->fd/dot_general | solution.py:140
  886.0 17.1 %convolution_multiply_fusion.1 = f32[2048,2048]{1,0:T(8,128)} fusion(f32[]{:T(128)S(6)} %div.63, bf16[1024,2048]{1,0:T(8,128)(2,1)} %copy-done.46, f32[1024,2048]{1,0:T(8,128)} %copy-done, f32[2048]{0:T(1024)S(1)} %bitcast.122, f32[2048]{0:T(1024)S(1)} %bitcast.98, f32[1024]{0:T(1024)S(1)} %fusion.42, f32[1024]{0:T(1024)S(1)} %broadcast_multiply_fusion.4), kind=kOutput, calls=%fused_computation.24 | convolution fusion | flops 8604614656 | bytes 29384708 | tf_op jit(solution)/shard_map/sd,sf->df/dot_general | solution.py:150
  904.4 13.7 broadcast_multiply_fusion
  918.8 8.9 all-gather.7
  930.4 242.6 %all-reduce.17.cloned.1.call-done = (bf16[1024,2048]{1,0:T(8,128)(2,1)}, bf16[1024,2048]{1,0:T(8,128)(2,1)}) async-done(((bf16[1024,2048]{1,0:T(8,128)(2,1)}, bf16[1024,2048]{1,0:T(8,128)(2,1)}), (bf16[1024,2048]{1,0:T(8,128)(2,1)}, bf16[1024,2048]{1,0:T(8,128)(2,1)})) %all-reduce.17.cloned.1.call-update) | async-done | bytes 8388624 | tf_op jit(solution)/shard_map/psum | solution.py:130
  1183.4 10.4 fusion.19
  1194.0 25.5 %all-reduce.7 = (f32[2048]{0:T(1024)S(1)}, f32[2048]{0:T(1024)S(1)}, f32[2048]{0:T(1024)S(1)}, f32[2048]{0:T(1024)S(1)}, f32[2048]{0:T(1024)S(1)}, /*index=5*/f32[2048]{0:T(1024)S(1)}, f32[2048]{0:T(1024)S(1)}) all-reduce(f32[2048]{0:T(1024)S(1)} %bitcast.111, f32[2048]{0:T(1024)S(1)} %bitcast.110, ...), channel_id=6, replica_groups=mesh['dp'=8,'mp'=4] {'dp'}, use_global_device_ids=true, to_apply=%region_26.27.clone | all-reduce | flops 14336 | bytes 114688
  1232.4 115.7 %reduce-scatter.14.cloned.1.call-done = f32[2048,256]{1,0:T(8,128)} async-done(((f32[2048,2048]{1,0:T(8,128)}), f32[2048,256]{1,0:T(8,128)}) %reduce-scatter.14.cloned.1.call-update) | async-done | bytes 2097168 | tf_op jit(solution)/shard_map/reduce_scatter | solution.py:211
  1348.0 120.2 %reduce-scatter.12.cloned.1.call-done = f32[256,2048]{1,0:T(8,128)} async-done(((f32[2048,2048]{1,0:T(8,128)}), f32[256,2048]{1,0:T(8,128)}) %reduce-scatter.12.cloned.1.call-update) | async-done | bytes 2097168 | tf_op jit(solution)/shard_map/reduce_scatter | solution.py:210
  1468.2 96.2 %reduce-scatter.8.cloned.1.call-done = f32[256,3,512]{2,0,1:T(8,128)} async-done(((f32[2048,3,512]{2,0,1:T(8,128)}), f32[256,3,512]{2,0,1:T(8,128)}) %reduce-scatter.8.cloned.1.call-update) | async-done | bytes 1572880 | tf_op jit(solution)/shard_map/reduce_scatter | solution.py:204
  (217 shorter events, 163.4 us)
Async XLA Ops:
  7.2 52.6 %all-gather.12.cloned.1.call-start = ((), (), s32[]{:S(2)}) async-start(), calls=%async_computation.5 | async-start | bytes 7077888 | tf_op jit(solution)/shard_map/all_gather | solution.py:73
  9.5 93.6 %all-gather.14.cloned.1.call-start = ((), (), s32[]{:S(2)}) async-start(), calls=%async_computation.6 | async-start | bytes 2359296 | tf_op jit(solution)/shard_map/all_gather | solution.py:74
  10.3 391.9 %all-reduce.13.cloned.1.call-start = ((), (), s32[]{:S(2)}) async-start(), calls=%async_computation.7 | async-start | bytes 16777216 | tf_op jit(solution)/shard_map/psum | solution.py:124
  22.4 49.7 %copy-start.32 = (f32[1,512]{1,0:T(1,128)}, f32[1,512]{1,0:T(1,128)S(1)}, u32[]{:S(2)}) copy-start(f32[1,512]{1,0:T(1,128)S(1)} %get-tuple-element.47) | copy-start | bytes 6148
  25.3 44.9 %copy-start.24 = (f32[1024]{0:T(1024)}, f32[1024]{0:T(1024)S(1)}, u32[]{:S(2)}) copy-start(f32[1024]{0:T(1024)S(1)} %broadcast_multiply_fusion.5) | copy-start | bytes 12292
  28.8 41.5 %copy-start.26 = (f32[1024]{0:T(1024)}, f32[1024]{0:T(1024)S(1)}, u32[]{:S(2)}) copy-start(f32[1024]{0:T(1024)S(1)} %fusion.41) | copy-start | bytes 12292
  37.7 32.6 %copy-start.34 = (f32[8,1,256]{2,1,0:T(1,128)}, f32[8,1,256]{2,1,0:T(1,128)S(1)}, u32[]{:S(2)}) copy-start(f32[8,1,256]{2,1,0:T(1,128)S(1)} %convert_element_type.130) | copy-start | bytes 24580
  46.3 23.9 %copy-start.22 = (f32[8,1,256]{2,1,0:T(1,128)}, f32[8,1,256]{2,1,0:T(1,128)S(1)}, u32[]{:S(2)}) copy-start(f32[8,1,256]{2,1,0:T(1,128)S(1)} %convert_element_type.129) | copy-start | bytes 24580
  103.1 59.7 %copy-start.40 = (bf16[256]{0:T(256)(128)(2,1)S(1)}, bf16[256]{0:T(256)(128)(2,1)}, u32[]{:S(2)}) copy-start(bf16[256]{0:T(256)(128)(2,1)} %param.24) | copy-start | bytes 1540
  103.1 59.6 %copy-start.41 = (bf16[256]{0:T(256)(128)(2,1)S(1)}, bf16[256]{0:T(256)(128)(2,1)}, u32[]{:S(2)}) copy-start(bf16[256]{0:T(256)(128)(2,1)} %param.25) | copy-start | bytes 1540
  103.1 59.7 %copy-start.42 = (bf16[256]{0:T(256)(128)(2,1)S(1)}, bf16[256]{0:T(256)(128)(2,1)}, u32[]{:S(2)}) copy-start(bf16[256]{0:T(256)(128)(2,1)} %param.27) | copy-start | bytes 1540
  103.1 59.7 %copy-start.43 = (bf16[256]{0:T(256)(128)(2,1)S(1)}, bf16[256]{0:T(256)(128)(2,1)}, u32[]{:S(2)}) copy-start(bf16[256]{0:T(256)(128)(2,1)} %param.28) | copy-start | bytes 1540
  103.2 101.3 %copy-start.39 = (s32[8]{0:T(128)S(1)}, s32[8]{0:T(128)}, u32[]{:S(2)}) copy-start(s32[8]{0:T(128)} %param.17) | copy-start | bytes 100
  111.0 347.8 %all-gather.16.cloned.1.call-start = ((), (), s32[]{:S(2)}) async-start(), calls=%async_computation.8 | async-start | bytes 9437184 | tf_op jit(solution)/shard_map/all_gather | solution.py:76
  111.5 674.0 %all-reduce.15.cloned.1.call-start = ((), (), s32[]{:S(2)}) async-start(), calls=%async_computation.9 | async-start | bytes 16777216 | tf_op jit(solution)/shard_map/psum | solution.py:154
  111.6 25.3 %collective-permute-start = (bf16[256,2048]{1,0:T(8,128)(2,1)S(1)}, bf16[256,2048]{1,0:T(8,128)(2,1)S(1)}, u32[]{:S(2)}, u32[]{:S(2)}) collective-permute-start(bf16[256,2048]{1,0:T(8,128)(2,1)S(1)} %copy-done.16), channel_id=1, source_target_pairs={{0,4},{4,8},{8,12},{12,16},{16,20},{20,24},{24,28},{28,0},{1,5},{5... | collective-permute-start | bytes 3145736 | tf_op jit(solution)/shard_map/ppermute | solution.py:21
  111.8 25.1 %collective-permute-start.1 = (bf16[256,2048]{1,0:T(8,128)(2,1)S(1)}, bf16[256,2048]{1,0:T(8,128)(2,1)S(1)}, u32[]{:S(2)}, u32[]{:S(2)}) collective-permute-start(bf16[256,2048]{1,0:T(8,128)(2,1)S(1)} %copy-done.16), channel_id=1, source_target_pairs={{0,28},{4,0},{8,4},{12,8},{16,12},{20,16},{24,20},{28,24},{1,29},{... | collective-permute-start | bytes 3145736 | tf_op jit(solution)/shard_map/ppermute | solution.py:26
  136.9 25.8 %collective-permute-start.2 = (bf16[256,2048]{1,0:T(8,128)(2,1)S(1)}, bf16[256,2048]{1,0:T(8,128)(2,1)}, u32[]{:S(2)}, u32[]{:S(2)}) collective-permute-start(bf16[256,2048]{1,0:T(8,128)(2,1)S(1)} %collective-permute-done), channel_id=1, source_target_pairs={{0,4},{4,8},{8,12},{12,16},{16,20},{20,24},{24,28},{28,0},{1,5},{5... | collective-permute-start | bytes 3145736 | tf_op jit(solution)/shard_map/ppermute | solution.py:21
  136.9 74.3 %collective-permute-start.3 = (bf16[256,2048]{1,0:T(8,128)(2,1)S(1)}, bf16[256,2048]{1,0:T(8,128)(2,1)}, u32[]{:S(2)}, u32[]{:S(2)}) collective-permute-start(bf16[256,2048]{1,0:T(8,128)(2,1)S(1)} %collective-permute-done.1), channel_id=1, source_target_pairs={{0,28},{4,0},{8,4},{12,8},{16,12},{20,16},{24,20},{28,24},{1,29},{... | collective-permute-start | bytes 3145736 | tf_op jit(solution)/shard_map/ppermute | solution.py:26
  162.8 50.9 %collective-permute-start.4 = (bf16[256,2048]{1,0:T(8,128)(2,1)}, bf16[256,2048]{1,0:T(8,128)(2,1)S(1)}, u32[]{:S(2)}, u32[]{:S(2)}) collective-permute-start(bf16[256,2048]{1,0:T(8,128)(2,1)} %collective-permute-done.2), channel_id=1, source_target_pairs={{0,4},{4,8},{8,12},{12,16},{16,20},{20,24},{24,28},{28,0},{1,5},{5... | collective-permute-start | bytes 3145736 | tf_op jit(solution)/shard_map/ppermute | solution.py:21
  196.7 212.2 %copy-start.36 = (f32[8,1,256]{2,1,0:T(1,128)}, f32[8,1,256]{2,1,0:T(1,128)S(1)}, u32[]{:S(2)}) copy-start(f32[8,1,256]{2,1,0:T(1,128)S(1)} %convert_element_type.134) | copy-start | bytes 24580
  211.2 24.4 %collective-permute-start.5 = (bf16[256,2048]{1,0:T(8,128)(2,1)}, bf16[256,2048]{1,0:T(8,128)(2,1)S(1)}, u32[]{:S(2)}, u32[]{:S(2)}) collective-permute-start(bf16[256,2048]{1,0:T(8,128)(2,1)} %collective-permute-done.3), channel_id=1, source_target_pairs={{0,28},{4,0},{8,4},{12,8},{16,12},{20,16},{24,20},{28,24},{1,29},{... | collective-permute-start | bytes 3145736 | tf_op jit(solution)/shard_map/ppermute | solution.py:26
  213.6 24.9 %collective-permute-start.6 = (bf16[256,2048]{1,0:T(8,128)(2,1)S(1)}, bf16[256,2048]{1,0:T(8,128)(2,1)S(1)}, u32[]{:S(2)}, u32[]{:S(2)}) collective-permute-start(bf16[256,2048]{1,0:T(8,128)(2,1)S(1)} %collective-permute-done.4), channel_id=1, source_target_pairs={{0,4},{4,8},{8,12},{12,16},{16,20},{20,24},{24,28},{28,0},{1,5},{5... | collective-permute-start | bytes 3145736 | tf_op jit(solution)/shard_map/ppermute | solution.py:21
  494.6 434.4 %reduce-scatter.16.cloned.1.call-start = ((), (), s32[]{:S(2)}) async-start(), calls=%async_computation.14 | async-start | bytes 294912
  819.1 12.4 copy-start.7
  819.1 12.4 copy-start.33
  846.1 326.9 %all-reduce.17.cloned.1.call-start = ((), (), s32[]{:S(2)}) async-start(), calls=%async_computation.15 | async-start | bytes 16777216 | tf_op jit(solution)/shard_map/psum | solution.py:130
  857.3 375.1 %reduce-scatter.10.cloned.1.call-start = ((), (), s32[]{:S(2)}) async-start(), calls=%async_computation.11 | async-start | bytes 4718592 | tf_op jit(solution)/shard_map/reduce_scatter | solution.py:205
  867.7 480.3 %reduce-scatter.14.cloned.1.call-start = ((), (), s32[]{:S(2)}) async-start(), calls=%async_computation.13 | async-start | bytes 18874368 | tf_op jit(solution)/shard_map/reduce_scatter | solution.py:211
  885.4 582.9 %reduce-scatter.12.cloned.1.call-start = ((), (), s32[]{:S(2)}) async-start(), calls=%async_computation.12 | async-start | bytes 18874368 | tf_op jit(solution)/shard_map/reduce_scatter | solution.py:210
  903.2 661.2 %reduce-scatter.8.cloned.1.call-start = ((), (), s32[]{:S(2)}) async-start(), calls=%async_computation.10 | async-start | bytes 14155776 | tf_op jit(solution)/shard_map/reduce_scatter | solution.py:204
  918.1 260.3 %copy-start.29 = (f32[1024]{0:T(1024)S(1)}, f32[1024]{0:T(1024)}, u32[]{:S(2)}) copy-start(f32[1024]{0:T(1024)} %copy-done.28) | copy-start | bytes 12292
  (35 other events, 196.8 us)
Sparse Core Ops, SparseCore 0:
  10.4 49.3 all-gather.11
  61.7 28.0 all-gather.13
  111.1 291.0 all-reduce.12
  403.9 54.8 all-gather.15
  494.7 290.8 all-reduce.14
  846.3 32.6 reduce-scatter.15
  882.1 290.8 all-reduce.16
  1177.0 50.8 reduce-scatter.9
  1232.0 115.9 reduce-scatter.13
  1352.0 116.1 reduce-scatter.11
  1472.3 92.0 reduce-scatter.7
